TPU v7x, 256 devices: a whole 4x4x8 slice. The times are simulated.
256 devices in a mesh: lat: 128 (over z, x, y), fld: 2 (over core).
Axes of the slice: x: 4, y: 4, z: 8, core: 2. Of those that a mesh axis runs over, the one named last changes fastest.
Arguments:
- grid_fields: bfloat16 [3, 16, 256, 2, 1152], P(None, 'fld', 'lat'), may hold values from -6 to 6
- legendre_basis: bfloat16 [640, 2, 256, 640], P('lat', 'fld'), may hold values from -0.25 to 0.25
- owner_list: int32 [640], replicated, may hold values from 0 to 639, as said below
- wave_speed: float32 [16], P('fld'), may hold values from 1e-06 to 0.01
Outputs:
- balanced_spectra: bfloat16 [640, 2, 3, 16, 640], P('lat', None, None, 'fld')
- balanced_grid: bfloat16 [3, 16, 256, 2, 1152], P(None, 'fld', 'lat')
Inputs may be any that keep to these rules, and one draw needn't show every extreme that they name: owner_list is a permutation of the 640 wavenumbers; slot d * 5 + r holds a wavenumber of r * 128 to r * 128 + 127, and for each index d of lat the slots of rounds 2 i and 2 i + 1 hold wavenumbers that add up to (4 i + 2) * 128 - 1.
All inputs are finite; a program needn't handle non-finite values.
Results may differ from a plain program's by a relative error of at most 0.0074.
Values may be sent and summed in bfloat16 or wider, within the bound.
No kernel may reach another device: no remote copies, remote signals or barrier semaphores. Data moves between devices by JAX's collectives and lax.ppermute only.
A program may use at most 128 MiB of HBM per device.

v0:
```python
import math

import jax
import jax.numpy as jnp
from jax import lax
from jax.experimental import pallas as pl
from jax.experimental.pallas import tpu as pltpu
from jax.sharding import PartitionSpec as P

F32 = jnp.float32
BF16 = jnp.bfloat16
LANES = 128
SINE_TERMS = (-1.0 / 6.0, 1.0 / 120.0, -1.0 / 5040.0, 1.0 / 362880.0)
COSINE_TERMS = (-1.0 / 2.0, 1.0 / 24.0, -1.0 / 720.0, 1.0 / 40320.0, -1.0 / 3628800.0)


def cosine_sine(product, quarters, quarter, turn):
    steps = jnp.floor(product * quarters + 0.5)
    angle = (product - steps * quarter) * turn
    square = angle * angle
    sine = F32(SINE_TERMS[-1])
    for term in SINE_TERMS[-2::-1]:
        sine = sine * square + F32(term)
    sine = angle + angle * square * sine
    cosine = F32(COSINE_TERMS[-1])
    for term in COSINE_TERMS[-2::-1]:
        cosine = cosine * square + F32(term)
    cosine = 1.0 + square * cosine
    quadrant = steps - 4.0 * jnp.floor(steps * 0.25)
    odd = (quadrant == 1.0) | (quadrant == 3.0)
    first = jnp.where(odd, sine, cosine)
    second = jnp.where(odd, cosine, sine)
    first = jnp.where((quadrant == 1.0) | (quadrant == 2.0), -first, first)
    second = jnp.where(quadrant >= 2.0, -second, second)
    return first, second


def analyse_kernel(position_ref, waves_ref, rows_ref, table_ref, out_ref, stage_ref):
    pair_count, lines, padded = rows_ref.shape
    half_lines = lines // 2
    rounds = table_ref.shape[1] // (2 * LANES)
    wave_count = rounds * LANES
    chunk = 32

    def build(step, carry):
        pair = step // rounds
        turn_round = step % rounds
        points = 20 + 4 * (position_ref[0] * pair_count + pair)
        highest = jnp.minimum(wave_count - 1, (points - 1) // 2).astype(F32)
        points_row = jnp.full((1, LANES), points.astype(F32), F32)
        quarters = 4.0 / points_row
        quarter = points_row * 0.25
        turn = F32(2.0 * math.pi) / points_row
        scaling = 1.0 / jnp.sqrt(points_row)
        waves_row = waves_ref[pl.ds(turn_round, 1), :]
        waves = jnp.transpose(jnp.broadcast_to(waves_row, (LANES, LANES)))
        for first in range(0, LANES, chunk):
            wave = waves[first : first + chunk]
            column = lax.broadcasted_iota(jnp.int32, (chunk, LANES), 1).astype(F32)
            cosine, sine = cosine_sine(wave * column, quarters, quarter, turn)
            shift_cosine, shift_sine = cosine_sine(wave * F32(LANES), quarters, quarter, turn)
            amplitude = jnp.where(wave <= highest, scaling, 0.0)
            real = cosine * amplitude
            imaginary = -sine * amplitude
            for block in range(padded // LANES):
                place = pl.ds(block * LANES, LANES)
                table_ref[pair, pl.ds(turn_round * LANES + first, chunk), place] = real.astype(BF16)
                table_ref[pair, pl.ds(wave_count + turn_round * LANES + first, chunk), place] = (
                    imaginary.astype(BF16)
                )
                if block + 1 < padded // LANES:
                    real, imaginary = (
                        real * shift_cosine + imaginary * shift_sine,
                        imaginary * shift_cosine - real * shift_sine,
                    )
        return carry

    lax.fori_loop(0, pair_count * rounds, build, 0)
    column = lax.broadcasted_iota(jnp.int32, (lines, padded), 1)
    spare = jnp.zeros((LANES - rounds * half_lines, LANES), F32)
    for pair in range(pair_count):
        points = 20 + 4 * (position_ref[0] * pair_count + pair)
        rows = jnp.where(column < points, rows_ref[pair].astype(F32), 0.0).astype(BF16)
        fourier = lax.dot_general(
            rows, table_ref[pair], (((1,), (1,)), ((), ())), preferred_element_type=F32
        )
        for part in range(2):
            for hemi in range(2):
                pieces = [
                    fourier[
                        hemi * half_lines : (hemi + 1) * half_lines,
                        part * wave_count + r * LANES : part * wave_count + (r + 1) * LANES,
                    ]
                    for r in range(rounds)
                ]
                packed = jnp.transpose(jnp.concatenate(pieces + [spare], axis=0))
                stage_ref[pl.ds(part * 4 + hemi * 2 + pair, LANES, stride=8), :] = packed
    out_ref[...] = stage_ref[...].astype(BF16)


def balance_kernel(
    hemi_ref, own_wave_ref, speeds_ref, got_ref, basis_ref, other_ref,
    balanced_ref, out_ref, stage_ref, line_ref, wide_ref,
):
    slot_count, half_count, totals_count = basis_ref.shape
    lines = balanced_ref.shape[0] // slot_count
    half_lines = lines // 2
    modes = speeds_ref.shape[0]
    hemi_own = hemi_ref[0]
    hemi_other = 1 - hemi_own
    stage_ref[...] = got_ref[...].astype(F32)
    for group in range(4):
        for pair in range(2):
            line_ref[group, pl.ds(pair, LANES, stride=2), :] = stage_ref[
                pl.ds(group * 2 + pair, LANES, stride=8), :
            ]
    own_rows = [jnp.transpose(line_ref[2 * part + hemi_own]) for part in range(2)]
    other_rows = [jnp.transpose(line_ref[2 * part + hemi_other]) for part in range(2)]

    totals = lax.broadcasted_iota(jnp.int32, (modes, totals_count), 1)
    degree = totals.astype(F32)
    stiffness = degree * (degree + 1.0) * speeds_ref[...]
    retained = 1.0 / (1.0 + stiffness)
    root_term = jnp.sqrt(stiffness)
    removed = stiffness * retained

    for r in range(slot_count):
        span = slice(r * half_lines, (r + 1) * half_lines)
        own = jnp.concatenate([own_rows[0][span], own_rows[1][span]], axis=0).astype(BF16)
        other = jnp.concatenate([other_rows[0][span], other_rows[1][span]], axis=0).astype(BF16)
        spectra = jnp.dot(own, basis_ref[r], preferred_element_type=F32) + jnp.dot(
            other, other_ref[r], preferred_element_type=F32
        )
        inside = totals >= own_wave_ref[r]
        pieces = []
        for part in range(2):
            base = part * half_lines
            vorticity = spectra[base : base + modes]
            divergence = spectra[base + modes : base + 2 * modes]
            geopotential = spectra[base + 2 * modes : base + 3 * modes]
            rossby_part = (root_term * vorticity - geopotential) * retained
            pieces.append(jnp.where(inside, retained * vorticity + removed * root_term * rossby_part, 0.0))
            pieces.append(jnp.where(inside, retained * divergence, 0.0))
            pieces.append(jnp.where(inside, retained * geopotential - removed * rossby_part, 0.0))
        result = jnp.concatenate(pieces, axis=0).astype(BF16)
        balanced_ref[r * lines : (r + 1) * lines, :] = result
        weight = jnp.where(own_wave_ref[r] == 0, 1.0, 2.0).astype(F32)
        scaled = result.astype(F32) * weight
        wide_ref[pl.ds(r * half_lines, half_lines), :] = scaled[:half_lines]
        wide_ref[pl.ds(LANES + r * half_lines, half_lines), :] = scaled[half_lines:]
    spare = LANES - slot_count * half_lines
    for part in range(2):
        wide_ref[pl.ds((part + 1) * LANES - spare, spare), :] = jnp.zeros((spare, totals_count), F32)

    tall = jnp.transpose(wide_ref[...])
    lane = lax.broadcasted_iota(jnp.int32, tall.shape, 1) % LANES
    own_sum = jnp.zeros((half_count, 2 * LANES), F32)
    other_sum = jnp.zeros((half_count, 2 * LANES), F32)
    for r in range(slot_count):
        chosen = (lane >= r * half_lines) & (lane < (r + 1) * half_lines)
        values = jnp.where(chosen, tall, 0.0).astype(BF16)
        own_sum += jnp.dot(basis_ref[r], values, preferred_element_type=F32)
        other_sum += jnp.dot(other_ref[r], values, preferred_element_type=F32)
    for part in range(2):
        line_ref[2 * part + hemi_own] = own_sum[:, part * LANES : (part + 1) * LANES]
        line_ref[2 * part + hemi_other] = other_sum[:, part * LANES : (part + 1) * LANES]
    for group in range(4):
        for pair in range(2):
            stage_ref[pl.ds(group * 2 + pair, LANES, stride=8), :] = line_ref[
                group, pl.ds(pair, LANES, stride=2), :
            ]
    out_ref[...] = stage_ref[...].astype(BF16)


def compose_kernel(position_ref, got_ref, table_ref, out_ref, stage_ref):
    pair_count, lines, padded = out_ref.shape
    half_lines = lines // 2
    rounds = table_ref.shape[1] // (2 * LANES)
    stage_ref[...] = got_ref[...].astype(F32)
    column = lax.broadcasted_iota(jnp.int32, (lines, padded), 1)
    for pair in range(pair_count):
        halves = []
        for hemi in range(2):
            pieces = []
            for part in range(2):
                slab = jnp.transpose(stage_ref[pl.ds(part * 4 + hemi * 2 + pair, LANES, stride=8), :])
                pieces += [slab[r * half_lines : (r + 1) * half_lines] for r in range(rounds)]
            halves.append(jnp.concatenate(pieces, axis=1))
        values = jnp.concatenate(halves, axis=0).astype(BF16)
        grid = jnp.dot(values, table_ref[pair], preferred_element_type=F32)
        points = 20 + 4 * (position_ref[0] * pair_count + pair)
        out_ref[pair] = jnp.where(column < points, grid, 0.0).astype(BF16)


def smem():
    return pl.BlockSpec(memory_space=pltpu.SMEM)


def vmem():
    return pl.BlockSpec(memory_space=pltpu.VMEM)


def per_device(grid_fields, legendre_basis, owner_list, wave_speed):
    field_count, mode_count, pair_count, hemis, padded = grid_fields.shape
    slot_count, _, half_count, totals_count = legendre_basis.shape
    wave_count = owner_list.shape[0]
    peers = wave_count // slot_count
    lines = field_count * mode_count * hemis
    position = lax.axis_index("lat").astype(jnp.int32)
    hemi = lax.axis_index("fld").astype(jnp.int32)
    position_one = position.reshape(1)
    basis = legendre_basis.reshape(slot_count, half_count, totals_count)
    other = lax.ppermute(basis, "fld", [(0, 1), (1, 0)])
    own_wave = lax.dynamic_slice_in_dim(owner_list, position * slot_count, slot_count)
    waves = jnp.pad(
        jnp.transpose(owner_list.reshape(peers, slot_count)).astype(F32), ((0, 8 - slot_count), (0, 0))
    )
    rows = jnp.transpose(grid_fields, (2, 3, 0, 1, 4)).reshape(pair_count, lines, padded)
    params = pltpu.CompilerParams(vmem_limit_bytes=48 << 20)
    exchange = jax.ShapeDtypeStruct((peers * 8, LANES), BF16)

    table, sent = pl.pallas_call(
        analyse_kernel,
        out_shape=(jax.ShapeDtypeStruct((pair_count, 2 * wave_count, padded), BF16), exchange),
        in_specs=[smem(), vmem(), vmem()],
        out_specs=(vmem(), vmem()),
        scratch_shapes=[pltpu.VMEM((peers * 8, LANES), F32)],
        compiler_params=params,
        name="row_analysis",
    )(position_one, waves, rows)
    got = lax.all_to_all(sent.reshape(peers, 8, LANES), "lat", 0, 0, tiled=True)
    balanced, returned = pl.pallas_call(
        balance_kernel,
        out_shape=(jax.ShapeDtypeStruct((slot_count * lines, totals_count), BF16), exchange),
        in_specs=[smem(), smem(), vmem(), vmem(), vmem(), vmem()],
        out_specs=(vmem(), vmem()),
        scratch_shapes=[
            pltpu.VMEM((peers * 8, LANES), F32),
            pltpu.VMEM((4, half_count, LANES), F32),
            pltpu.VMEM((2 * LANES, totals_count), F32),
        ],
        compiler_params=params,
        name="legendre_balance",
    )(hemi.reshape(1), own_wave, wave_speed.reshape(mode_count, 1), got.reshape(peers * 8, LANES), basis, other)
    back = lax.all_to_all(returned.reshape(peers, 8, LANES), "lat", 0, 0, tiled=True)
    grid = pl.pallas_call(
        compose_kernel,
        out_shape=jax.ShapeDtypeStruct((pair_count, lines, padded), BF16),
        in_specs=[smem(), vmem(), vmem()],
        out_specs=vmem(),
        scratch_shapes=[pltpu.VMEM((peers * 8, LANES), F32)],
        compiler_params=params,
        name="row_synthesis",
    )(position_one, back.reshape(peers * 8, LANES), table)
    balanced_grid = jnp.transpose(
        grid.reshape(pair_count, hemis, field_count, mode_count, padded), (2, 3, 0, 1, 4)
    )
    balanced_spectra = balanced.reshape(slot_count, 2, field_count, mode_count, totals_count)
    return (balanced_spectra, balanced_grid)


def solution(mesh):
    placed = (P(None, "fld", "lat", None, None), P("lat", "fld", None, None), P(), P("fld"))
    return jax.shard_map(
        per_device,
        mesh=mesh,
        in_specs=placed,
        out_specs=(P("lat", None, None, "fld", None), P(None, "fld", "lat", None, None)),
        check_vma=False,
    )
```

profile of v0, /device:TPU:2, one launch (start us, length us, event | category | flops | bytes accessed | tf_op | source)
XLA Modules:
  0.0 70.9 jit_solution(13188546860620230860)
XLA Ops:
  0.6 0.1 collective-permute-start
  0.7 0.7 convert_element_type.11
  1.4 0.2 convert_element_type.12
  1.6 0.1 copy.9
  1.7 1.0 %copy.10 = bf16[2,2,3,8,1152]{4,3,2,1,0:T(8,128)(2,1)S(1)} copy(bf16[2,2,3,8,1152]{4,1,0,3,2:T(2,128)(2,1)} %bitcast.23) | data formatting | bytes 442368 | tf_op jit(solution)/shard_map/transpose | solution.py:218
  2.7 8.6 %row_analysis.1 = (bf16[2,1280,1152]{2,1,0:T(8,128)(2,1)}, bf16[1024,128]{1,0:T(8,128)(2,1)}) custom-call(s32[1]{0:T(128)} %bitcast.2.position_ref, f32[8,128]{1,0:T(8,128)S(1)} %pad.4.waves_ref, bf16[2,48,1152]{2,1,0:T(8,128)(2,1)S(1)} %bitcast.20), custom_call_target="tpu_custom_call" | custom-call | tf_op jit(solution)/shard_map/row_analysis/pallas_call | solution.py:222
  11.2 15.4 %all-to-all-start = ((bf16[128,8,128]{2,1,0:T(8,128)(2,1)}), bf16[128,8,128]{2,1,0:T(8,128)(2,1)S(1)}, u32[]{:S(2)}, u32[]{:S(2)}) async-start(bf16[128,8,128]{2,1,0:T(8,128)(2,1)} %bitcast.6), calls=%async_computation | async-start | bytes 524288 | tf_op jit(solution)/shard_map/all_to_all | solution.py:231
  26.7 0.8 %dynamic_slice.3.own_wave_ref = s32[5]{0:T(128)S(1)} dynamic-slice(s32[640]{0:T(1024)} %param.6, s32[]{:T(128)S(6)} %select_n.3), dynamic_slice_sizes={5} | dynamic-slice | bytes 44 | tf_op jit(solution)/shard_map/dynamic_slice | solution.py:214
  27.4 0.7 %copy.11.speeds_ref = f32[8,1]{1,0:T(8,128)S(1)} copy(f32[8,1]{0,1:T(1,128)} %bitcast.26) | data formatting | bytes 64 | tf_op jit(solution)/shard_map/reshape | solution.py:244
  28.2 13.8 %all-to-all-done = bf16[128,8,128]{2,1,0:T(8,128)(2,1)S(1)} async-done(((bf16[128,8,128]{2,1,0:T(8,128)(2,1)}), bf16[128,8,128]{2,1,0:T(8,128)(2,1)S(1)}, u32[]{:S(2)}, u32[]{:S(2)}) %all-to-all-start) | async-done | bytes 262176 | tf_op jit(solution)/shard_map/all_to_all | solution.py:231
  42.0 0.0 collective-permute-done.other_ref
  42.0 0.0 copy-start
  42.0 1.4 %copy-done = bf16[5,1,256,640]{3,2,1,0:T(8,128)(2,1)S(1)} copy-done((bf16[5,1,256,640]{3,2,1,0:T(8,128)(2,1)S(1)}, bf16[5,1,256,640]{3,2,1,0:T(8,128)(2,1)}, u32[]{:S(2)}) %copy-start) | copy-done | bytes 1638424
  43.4 3.1 %legendre_balance.1 = (bf16[240,640]{1,0:T(8,128)(2,1)}, bf16[1024,128]{1,0:T(8,128)(2,1)S(1)}) custom-call(s32[1]{0:T(128)} %bitcast.hemi_ref, s32[5]{0:T(128)S(1)} %dynamic_slice.3.own_wave_ref, f32[8,1]{1,0:T(8,128)S(1)} %copy.11.speeds_ref, bf16[1024,128]{1,0:T(8,128)(2,1)S(1)} %bitcast.18, bf16[5,256,640]{2,1,0:T(8,128)(2,1)S(1)} %bitcast.17, ...), custom_call_target="tpu_custom_call" | custom-call | tf_op jit(solution)/shard_map/legendre_balance/pallas_call | solution.py:232
  46.5 19.8 %all_to_all.10 = bf16[128,8,128]{2,1,0:T(8,128)(2,1)S(1)} all-to-all(bf16[128,8,128]{2,1,0:T(8,128)(2,1)S(1)} %bitcast.22), channel_id=1, replica_groups=mesh['lat'=128,'fld'=2] {'lat'}, dimensions={0} | all-to-all | bytes 524288 | tf_op jit(solution)/shard_map/all_to_all | solution.py:245
  66.3 3.8 %row_synthesis.1 = bf16[2,48,1152]{2,1,0:T(8,128)(2,1)S(1)} custom-call(s32[1]{0:T(128)} %bitcast.2.position_ref, bf16[1024,128]{1,0:T(8,128)(2,1)S(1)} %bitcast.19, bf16[2,1280,1152]{2,1,0:T(8,128)(2,1)} %get-tuple-element.9.table_ref), custom_call_target="tpu_custom_call" | custom-call | tf_op jit(solution)/shard_map/row_synthesis/pallas_call | solution.py:246
  70.1 0.9 %copy.14 = bf16[2,2,3,8,1152]{4,1,0,3,2:T(2,128)(2,1)} copy(bf16[2,2,3,8,1152]{4,3,2,1,0:T(8,128)(2,1)S(1)} %bitcast.21) | data formatting | bytes 442368 | tf_op jit(solution)/shard_map/reshape | solution.py:256
  (1 shorter events, 0.0 us)
Async XLA Ops:
  0.6 41.3 %collective-permute-start = (bf16[5,256,640]{2,1,0:T(8,128)(2,1)}, bf16[5,256,640]{2,1,0:T(8,128)(2,1)S(1)}, u32[]{:S(2)}, u32[]{:S(2)}) collective-permute-start(bf16[5,256,640]{2,1,0:T(8,128)(2,1)} %bitcast.16), channel_id=1, source_target_pairs={{0,1},{1,0},{2,3},{3,2},{4,5},{5,4},{6,7},{7,6},{8,9},{9,8},{10,11... | collective-permute-start | bytes 4915208 | tf_op jit(solution)/shard_map/ppermute | solution.py:213
  11.2 30.7 %all-to-all-start = ((bf16[128,8,128]{2,1,0:T(8,128)(2,1)}), bf16[128,8,128]{2,1,0:T(8,128)(2,1)S(1)}, u32[]{:S(2)}, u32[]{:S(2)}) async-start(bf16[128,8,128]{2,1,0:T(8,128)(2,1)} %bitcast.6), calls=%async_computation | async-start | bytes 524288 | tf_op jit(solution)/shard_map/all_to_all | solution.py:231
  42.0 1.4 %copy-start = (bf16[5,1,256,640]{3,2,1,0:T(8,128)(2,1)S(1)}, bf16[5,1,256,640]{3,2,1,0:T(8,128)(2,1)}, u32[]{:S(2)}) copy-start(bf16[5,1,256,640]{3,2,1,0:T(8,128)(2,1)} %param.5) | copy-start | bytes 4915204
where the time goes:
time: 71.3 us; the launch traced here: 70.9 us
  blocking collectives  19.8 us (28%)
  starting transfers between devices  15.5 us (22%)
  Pallas kernels  15.4 us (22%)
  waiting for transfers between devices  13.8 us (19%)
  local copies, waits for them, and re-layouts  5.03 us (7%)
    all_to_all x1, blocking collectives, per_device(): lax.all_to_all(returned.reshape(peers, 8, LANES), 'lat', 0, 0, tiled=True)  19.8 us
    all_to_all x1, starting transfers between devices, per_device(): got = lax.all_to_all(sent.reshape(peers, 8, LANES), 'lat', 0, 0, tiled=True)  15.4 us
    all_to_all x1, waiting for transfers between devices, per_device(): got = lax.all_to_all(sent.reshape(peers, 8, LANES), 'lat', 0, 0, tiled=True)  13.8 us
    pallas_call x1, Pallas kernels, per_device(): pl.pallas_call(analyse_kernel, out_shape=(jax.ShapeDtypeStruct((pair_coun...  8.55 us
    pallas_call x1, Pallas kernels, per_device(): pl.pallas_call(compose_kernel, out_shape=jax.ShapeDtypeStruct((pair_count...  3.75 us
    pallas_call x1, Pallas kernels, per_device(): pl.pallas_call(balance_kernel, out_shape=(jax.ShapeDtypeStruct((slot_coun...  3.08 us
    unnamed x2, local copies, waits for them, and re-layouts  1.43 us
  transfers between devices with their start and end apart: 2, of which 1 were waited for; matrix products, arithmetic and copies ran while one was open for 5% of the time, Pallas kernels for 12%

commit v1 on v0

--- a/solution.py
+++ b/solution.py
@@ -35,62 +35,91 @@
     return first, second
 
 
-def analyse_kernel(position_ref, waves_ref, rows_ref, table_ref, out_ref, stage_ref):
+def mirror_blocks(values):
+    row = lax.broadcasted_iota(jnp.int32, (LANES, LANES), 0)
+    column = lax.broadcasted_iota(jnp.int32, (LANES, LANES), 1)
+    flip = jnp.where(row + column == LANES - 1, 1.0, 0.0).astype(BF16)
+    blocks = values.shape[1] // LANES
+    pieces = [
+        jnp.dot(values[:, k * LANES : (k + 1) * LANES], flip, preferred_element_type=F32)
+        for k in reversed(range(blocks))
+    ]
+    return jnp.concatenate(pieces, axis=1)
+
+
+def row_constants(points):
+    points_row = jnp.full((1, LANES), points.astype(F32), F32)
+    return 4.0 / points_row, points_row * 0.25, F32(2.0 * math.pi) / points_row, 1.0 / jnp.sqrt(points_row)
+
+
+def analyse_kernel(position_ref, waves_ref, rows_ref, table_ref, out_ref, stage_ref, wave_ref):
     pair_count, lines, padded = rows_ref.shape
     half_lines = lines // 2
-    rounds = table_ref.shape[1] // (2 * LANES)
+    rounds = waves_ref.shape[0]
     wave_count = rounds * LANES
+    width = table_ref.shape[2]
     chunk = 32
-
-    def build(step, carry):
-        pair = step // rounds
-        turn_round = step % rounds
-        points = 20 + 4 * (position_ref[0] * pair_count + pair)
-        highest = jnp.minimum(wave_count - 1, (points - 1) // 2).astype(F32)
-        points_row = jnp.full((1, LANES), points.astype(F32), F32)
-        quarters = 4.0 / points_row
-        quarter = points_row * 0.25
-        turn = F32(2.0 * math.pi) / points_row
-        scaling = 1.0 / jnp.sqrt(points_row)
-        waves_row = waves_ref[pl.ds(turn_round, 1), :]
-        waves = jnp.transpose(jnp.broadcast_to(waves_row, (LANES, LANES)))
+    all_points = [20 + 4 * (position_ref[0] * pair_count + pair) for pair in range(pair_count)]
+
+    flat = jnp.concatenate([waves_ref[...].astype(F32), jnp.zeros((8 - rounds, LANES), F32)], axis=0)
+    quantities = [flat]
+    for points in all_points:
+        quarters, quarter, turn, _ = row_constants(points)
+        quantities += cosine_sine(flat * F32(LANES), quarters, quarter, turn)
+    filler = jnp.zeros((LANES - 8 * len(quantities), LANES), F32)
+    columns = jnp.transpose(jnp.concatenate(quantities + [filler], axis=0))
+    for r in range(rounds):
+        wave_ref[r * LANES : (r + 1) * LANES, :] = columns if r == 0 else pltpu.roll(columns, LANES - r, 1)
+
+    column = lax.broadcasted_iota(jnp.int32, (chunk, LANES), 1).astype(F32)
+    for r in range(rounds):
+        mine = wave_ref[pl.ds(r, LANES, stride=rounds), :]
         for first in range(0, LANES, chunk):
-            wave = waves[first : first + chunk]
-            column = lax.broadcasted_iota(jnp.int32, (chunk, LANES), 1).astype(F32)
-            cosine, sine = cosine_sine(wave * column, quarters, quarter, turn)
-            shift_cosine, shift_sine = cosine_sine(wave * F32(LANES), quarters, quarter, turn)
-            amplitude = jnp.where(wave <= highest, scaling, 0.0)
-            real = cosine * amplitude
-            imaginary = -sine * amplitude
-            for block in range(padded // LANES):
-                place = pl.ds(block * LANES, LANES)
-                table_ref[pair, pl.ds(turn_round * LANES + first, chunk), place] = real.astype(BF16)
-                table_ref[pair, pl.ds(wave_count + turn_round * LANES + first, chunk), place] = (
-                    imaginary.astype(BF16)
-                )
-                if block + 1 < padded // LANES:
-                    real, imaginary = (
-                        real * shift_cosine + imaginary * shift_sine,
-                        imaginary * shift_cosine - real * shift_sine,
-                    )
-        return carry
-
-    lax.fori_loop(0, pair_count * rounds, build, 0)
-    column = lax.broadcasted_iota(jnp.int32, (lines, padded), 1)
+            part = mine[first : first + chunk]
+            wave = jnp.broadcast_to(part[:, 0:1], (chunk, LANES))
+            for pair in range(pair_count):
+                points = all_points[pair]
+                quarters, quarter, turn, scaling = row_constants(points)
+                highest = jnp.minimum(wave_count - 1, (points - 1) // 2).astype(F32)
+                spot = 8 + 16 * pair
+                shift_cosine = jnp.broadcast_to(part[:, spot : spot + 1], (chunk, LANES))
+                shift_sine = jnp.broadcast_to(part[:, spot + 8 : spot + 9], (chunk, LANES))
+                cosine, sine = cosine_sine(wave * column, quarters, quarter, turn)
+                amplitude = jnp.where(wave <= highest, scaling, 0.0)
+                real = cosine * amplitude
+                imaginary = -sine * amplitude
+                top = r * LANES + first
+                for block in range(width // LANES):
+                    place = slice(block * LANES, (block + 1) * LANES)
+                    table_ref[pair, top : top + chunk, place] = real.astype(BF16)
+                    table_ref[pair, wave_count + top : wave_count + top + chunk, place] = imaginary.astype(BF16)
+                    if block + 1 < width // LANES:
+                        real, imaginary = (
+                            real * shift_cosine + imaginary * shift_sine,
+                            imaginary * shift_cosine - real * shift_sine,
+                        )
+
+    place = lax.broadcasted_iota(jnp.int32, (lines, width), 1)
     spare = jnp.zeros((LANES - rounds * half_lines, LANES), F32)
     for pair in range(pair_count):
-        points = 20 + 4 * (position_ref[0] * pair_count + pair)
-        rows = jnp.where(column < points, rows_ref[pair].astype(F32), 0.0).astype(BF16)
-        fourier = lax.dot_general(
-            rows, table_ref[pair], (((1,), (1,)), ((), ())), preferred_element_type=F32
-        )
-        for part in range(2):
+        points = all_points[pair]
+        middle = points // 2
+        mirrored = pltpu.roll(mirror_blocks(rows_ref[pair]), points + 1, 1)[:, :width]
+        rows = rows_ref[pair, :, :width].astype(F32)
+        between = (place >= 1) & (place < middle)
+        even = rows + jnp.where(between, mirrored, 0.0)
+        even = jnp.where(place <= middle, even, 0.0).astype(BF16)
+        odd = jnp.where(between, rows - mirrored, 0.0).astype(BF16)
+        for part, folded in enumerate((even, odd)):
+            fourier = lax.dot_general(
+                folded,
+                table_ref[pair, part * wave_count : (part + 1) * wave_count, :],
+                (((1,), (1,)), ((), ())),
+                preferred_element_type=F32,
+            )
             for hemi in range(2):
                 pieces = [
-                    fourier[
-                        hemi * half_lines : (hemi + 1) * half_lines,
-                        part * wave_count + r * LANES : part * wave_count + (r + 1) * LANES,
-                    ]
+                    fourier[hemi * half_lines : (hemi + 1) * half_lines, r * LANES : (r + 1) * LANES]
                     for r in range(rounds)
                 ]
                 packed = jnp.transpose(jnp.concatenate(pieces + [spare], axis=0))
@@ -99,9 +128,11 @@
 
 
 def balance_kernel(
-    hemi_ref, own_wave_ref, speeds_ref, got_ref, basis_ref, other_ref,
-    balanced_ref, out_ref, stage_ref, line_ref, wide_ref,
+    hemi_ref, own_wave_ref, speeds_ref, got_ref, basis_hbm, other_ref,
+    balanced_ref, out_ref, stage_ref, line_ref, wide_ref, basis_ref, arrived,
 ):
+    fetch = pltpu.make_async_copy(basis_hbm, basis_ref, arrived)
+    fetch.start()
     slot_count, half_count, totals_count = basis_ref.shape
     lines = balanced_ref.shape[0] // slot_count
     half_lines = lines // 2
@@ -124,6 +155,7 @@
     root_term = jnp.sqrt(stiffness)
     removed = stiffness * retained
 
+    fetch.wait()
     for r in range(slot_count):
         span = slice(r * half_lines, (r + 1) * half_lines)
         own = jnp.concatenate([own_rows[0][span], own_rows[1][span]], axis=0).astype(BF16)
@@ -175,21 +207,37 @@
 def compose_kernel(position_ref, got_ref, table_ref, out_ref, stage_ref):
     pair_count, lines, padded = out_ref.shape
     half_lines = lines // 2
-    rounds = table_ref.shape[1] // (2 * LANES)
+    wave_count = table_ref.shape[1] // 2
+    width = table_ref.shape[2]
+    rounds = wave_count // LANES
     stage_ref[...] = got_ref[...].astype(F32)
-    column = lax.broadcasted_iota(jnp.int32, (lines, padded), 1)
+    place = lax.broadcasted_iota(jnp.int32, (lines, padded), 1)
+    tail = jnp.zeros((lines, padded - width), F32)
     for pair in range(pair_count):
-        halves = []
-        for hemi in range(2):
-            pieces = []
-            for part in range(2):
+        waves = []
+        for part in range(2):
+            halves = []
+            for hemi in range(2):
                 slab = jnp.transpose(stage_ref[pl.ds(part * 4 + hemi * 2 + pair, LANES, stride=8), :])
-                pieces += [slab[r * half_lines : (r + 1) * half_lines] for r in range(rounds)]
-            halves.append(jnp.concatenate(pieces, axis=1))
-        values = jnp.concatenate(halves, axis=0).astype(BF16)
-        grid = jnp.dot(values, table_ref[pair], preferred_element_type=F32)
+                pieces = [slab[r * half_lines : (r + 1) * half_lines] for r in range(rounds)]
+                halves.append(jnp.concatenate(pieces, axis=1))
+            values = jnp.concatenate(halves, axis=0).astype(BF16)
+            waves.append(
+                jnp.dot(
+                    values,
+                    table_ref[pair, part * wave_count : (part + 1) * wave_count, :],
+                    preferred_element_type=F32,
+                )
+            )
+        even, odd = waves
         points = 20 + 4 * (position_ref[0] * pair_count + pair)
-        out_ref[pair] = jnp.where(column < points, grid, 0.0).astype(BF16)
+        turned = mirror_blocks((even - odd).astype(BF16))
+        shift = points + padded - width + 1
+        shift = jnp.where(shift >= padded, shift - padded, shift)
+        far = pltpu.roll(jnp.concatenate([turned, tail], axis=1), shift, 1)
+        near = jnp.concatenate([even + odd, tail], axis=1)
+        grid = jnp.where(place <= points // 2, near, far)
+        out_ref[pair] = jnp.where(place < points, grid, 0.0).astype(BF16)
 
 
 def smem():
@@ -212,19 +260,18 @@
     basis = legendre_basis.reshape(slot_count, half_count, totals_count)
     other = lax.ppermute(basis, "fld", [(0, 1), (1, 0)])
     own_wave = lax.dynamic_slice_in_dim(owner_list, position * slot_count, slot_count)
-    waves = jnp.pad(
-        jnp.transpose(owner_list.reshape(peers, slot_count)).astype(F32), ((0, 8 - slot_count), (0, 0))
-    )
+    waves = owner_list.reshape(slot_count, peers)
+    width = (padded // 2 + LANES - 1) // LANES * LANES
     rows = jnp.transpose(grid_fields, (2, 3, 0, 1, 4)).reshape(pair_count, lines, padded)
-    params = pltpu.CompilerParams(vmem_limit_bytes=48 << 20)
+    params = pltpu.CompilerParams(vmem_limit_bytes=24 << 20)
     exchange = jax.ShapeDtypeStruct((peers * 8, LANES), BF16)
 
     table, sent = pl.pallas_call(
         analyse_kernel,
-        out_shape=(jax.ShapeDtypeStruct((pair_count, 2 * wave_count, padded), BF16), exchange),
+        out_shape=(jax.ShapeDtypeStruct((pair_count, 2 * wave_count, width), BF16), exchange),
         in_specs=[smem(), vmem(), vmem()],
         out_specs=(vmem(), vmem()),
-        scratch_shapes=[pltpu.VMEM((peers * 8, LANES), F32)],
+        scratch_shapes=[pltpu.VMEM((peers * 8, LANES), F32), pltpu.VMEM((wave_count, LANES), F32)],
         compiler_params=params,
         name="row_analysis",
     )(position_one, waves, rows)
@@ -232,12 +279,14 @@
     balanced, returned = pl.pallas_call(
         balance_kernel,
         out_shape=(jax.ShapeDtypeStruct((slot_count * lines, totals_count), BF16), exchange),
-        in_specs=[smem(), smem(), vmem(), vmem(), vmem(), vmem()],
+        in_specs=[smem(), smem(), vmem(), vmem(), pl.BlockSpec(memory_space=pltpu.MemorySpace.HBM), vmem()],
         out_specs=(vmem(), vmem()),
         scratch_shapes=[
             pltpu.VMEM((peers * 8, LANES), F32),
             pltpu.VMEM((4, half_count, LANES), F32),
             pltpu.VMEM((2 * LANES, totals_count), F32),
+            pltpu.VMEM((slot_count, half_count, totals_count), BF16),
+            pltpu.SemaphoreType.DMA,
         ],
         compiler_params=params,
         name="legendre_balance",

time: 71.3 us -> 64.5 us (0.905)
  Pallas kernels: 15.4 us -> 8.22 us
  local copies, waits for them, and re-layouts: 5.03 us -> 6.12 us
    pallas_call x1, Pallas kernels: 8.55 us -> 3.08 us  [per_device(): pl.pallas_call(analyse_kernel, out_shape=(jax.ShapeDtypeStruct((pair_coun...]
    pallas_call x1, Pallas kernels: 3.75 us -> 1.15 us  [per_device(): pl.pallas_call(compose_kernel, out_shape=jax.ShapeDtypeStruct((pair_count...]
    unnamed x2 -> x6, local copies, waits for them, and re-layouts: 1.43 us -> 2.81 us
    pallas_call x1, Pallas kernels: 3.08 us -> 3.99 us  [per_device(): pl.pallas_call(balance_kernel, out_shape=(jax.ShapeDtypeStruct((slot_coun...]
  transfers between devices with their start and end apart: 2 -> 2, of which waited for: 1 -> 1; matrix products, arithmetic and copies ran while one was open for 5% -> 4% of each run, Pallas kernels for 12% -> 5%
where the time goes in v1:
time: 64.5 us; the launch traced here: 64.2 us
  blocking collectives  19.8 us (31%)
  starting transfers between devices  15.5 us (24%)
  waiting for transfers between devices  13.8 us (21%)
  Pallas kernels  8.22 us (13%)
  local copies, waits for them, and re-layouts  6.12 us (9%)
  between operations  0.7 us (1%)
    all_to_all x1, blocking collectives, per_device(): lax.all_to_all(returned.reshape(peers, 8, LANES), 'lat', 0, 0, tiled=True)  19.8 us
    all_to_all x1, starting transfers between devices, per_device(): got = lax.all_to_all(sent.reshape(peers, 8, LANES), 'lat', 0, 0, tiled=True)  15.4 us
    all_to_all x1, waiting for transfers between devices, per_device(): got = lax.all_to_all(sent.reshape(peers, 8, LANES), 'lat', 0, 0, tiled=True)  13.8 us
    pallas_call x1, Pallas kernels, per_device(): pl.pallas_call(balance_kernel, out_shape=(jax.ShapeDtypeStruct((slot_coun...  3.99 us
    pallas_call x1, Pallas kernels, per_device(): pl.pallas_call(analyse_kernel, out_shape=(jax.ShapeDtypeStruct((pair_coun...  3.08 us
    unnamed x6, local copies, waits for them, and re-layouts  2.81 us
  transfers between devices with their start and end apart: 2, of which 1 were waited for; matrix products, arithmetic and copies ran while one was open for 4% of the time, Pallas kernels for 5%

profile of v1, /device:TPU:2, one launch (start us, length us, event | category | flops | bytes accessed | tf_op | source)
XLA Modules:
  0.0 64.2 jit_solution(16963604152286990680)
XLA Ops:
  0.6 0.1 collective-permute-start
  0.7 1.0 %copy.6 = bf16[2,2,3,8,1152]{4,3,2,1,0:T(8,128)(2,1)S(1)} copy(bf16[2,2,3,8,1152]{4,1,0,3,2:T(2,128)(2,1)} %bitcast.25) | data formatting | bytes 442368 | tf_op jit(solution)/shard_map/transpose | solution.py:265
  1.7 0.0 copy-start.2
  1.7 0.7 %copy-done.2 = s32[640]{0:T(1024)S(1)} copy-done((s32[640]{0:T(1024)S(1)}, s32[640]{0:T(1024)}, u32[]{:S(2)}) %copy-start.2) | copy-done | bytes 2584
  2.4 3.1 %row_analysis.1 = (bf16[2,1280,640]{2,1,0:T(8,128)(2,1)S(1)}, bf16[1024,128]{1,0:T(8,128)(2,1)S(1)}) custom-call(s32[1]{0:T(128)} %bitcast.2.position_ref, s32[5,128]{1,0:T(8,128)S(1)} %bitcast.24, bf16[2,48,1152]{2,1,0:T(8,128)(2,1)S(1)} %bitcast.20), custom_call_target="tpu_custom_call" | custom-call | tf_op jit(solution)/shard_map/row_analysis/pallas_call | solution.py:269
  5.5 0.0 copy-start.1
  5.5 0.7 %copy-done.1 = bf16[1024,128]{1,0:T(8,128)(2,1)} copy-done((bf16[1024,128]{1,0:T(8,128)(2,1)}, bf16[1024,128]{1,0:T(8,128)(2,1)S(1)}, u32[]{:S(2)}) %copy-start.1) | copy-done | bytes 262168
  6.2 15.4 %all-to-all-start = ((bf16[128,8,128]{2,1,0:T(8,128)(2,1)}), bf16[128,8,128]{2,1,0:T(8,128)(2,1)S(1)}, u32[]{:S(2)}, u32[]{:S(2)}) async-start(bf16[128,8,128]{2,1,0:T(8,128)(2,1)} %bitcast.22), calls=%async_computation | async-start | bytes 524288 | tf_op jit(solution)/shard_map/all_to_all | solution.py:278
  21.6 0.8 %dynamic_slice.3.own_wave_ref = s32[5]{0:T(128)S(1)} dynamic-slice(s32[640]{0:T(1024)} %param.6, s32[]{:T(128)S(6)} %select_n.3), dynamic_slice_sizes={5} | dynamic-slice | bytes 44 | tf_op jit(solution)/shard_map/dynamic_slice | solution.py:262
  22.4 0.7 %copy.7.speeds_ref = f32[8,1]{1,0:T(8,128)S(1)} copy(f32[8,1]{0,1:T(1,128)} %bitcast.27) | data formatting | bytes 64 | tf_op jit(solution)/shard_map/reshape | solution.py:293
  23.1 13.8 %all-to-all-done = bf16[128,8,128]{2,1,0:T(8,128)(2,1)S(1)} async-done(((bf16[128,8,128]{2,1,0:T(8,128)(2,1)}), bf16[128,8,128]{2,1,0:T(8,128)(2,1)S(1)}, u32[]{:S(2)}, u32[]{:S(2)}) %all-to-all-start) | async-done | bytes 262176 | tf_op jit(solution)/shard_map/all_to_all | solution.py:278
  36.9 0.0 collective-permute-done.other_ref
  36.9 0.0 copy-start
  36.9 1.4 %copy-done = bf16[5,1,256,640]{3,2,1,0:T(8,128)(2,1)S(1)} copy-done((bf16[5,1,256,640]{3,2,1,0:T(8,128)(2,1)S(1)}, bf16[5,1,256,640]{3,2,1,0:T(8,128)(2,1)}, u32[]{:S(2)}) %copy-start) | copy-done | bytes 1638424
  38.4 4.0 %legendre_balance.1 = (bf16[240,640]{1,0:T(8,128)(2,1)}, bf16[1024,128]{1,0:T(8,128)(2,1)S(1)}) custom-call(s32[1]{0:T(128)} %bitcast.hemi_ref, s32[5]{0:T(128)S(1)} %dynamic_slice.3.own_wave_ref, f32[8,1]{1,0:T(8,128)S(1)} %copy.7.speeds_ref, bf16[1024,128]{1,0:T(8,128)(2,1)S(1)} %bitcast.18, bf16[5,256,640]{2,1,0:T(8,128)(2,1)S(1)} %bitcast.17, ...), custom_call_target="tpu_custom_call" | custom-call | tf_op jit(solution)/shard_map/legendre_balance/pallas_call | solution.py:279
  42.3 19.8 %all_to_all.10 = bf16[128,8,128]{2,1,0:T(8,128)(2,1)S(1)} all-to-all(bf16[128,8,128]{2,1,0:T(8,128)(2,1)S(1)} %bitcast.23), channel_id=1, replica_groups=mesh['lat'=128,'fld'=2] {'lat'}, dimensions={0} | all-to-all | bytes 524288 | tf_op jit(solution)/shard_map/all_to_all | solution.py:294
  62.2 1.1 %row_synthesis.1 = bf16[2,48,1152]{2,1,0:T(8,128)(2,1)S(1)} custom-call(s32[1]{0:T(128)} %bitcast.2.position_ref, bf16[1024,128]{1,0:T(8,128)(2,1)S(1)} %bitcast.19, bf16[2,1280,640]{2,1,0:T(8,128)(2,1)S(1)} %get-tuple-element.9.table_ref), custom_call_target="tpu_custom_call" | custom-call | tf_op jit(solution)/shard_map/row_synthesis/pallas_call | solution.py:295
  63.3 0.9 %copy.10 = bf16[2,2,3,8,1152]{4,1,0,3,2:T(2,128)(2,1)} copy(bf16[2,2,3,8,1152]{4,3,2,1,0:T(8,128)(2,1)S(1)} %bitcast.21) | data formatting | bytes 442368 | tf_op jit(solution)/shard_map/reshape | solution.py:305
Async XLA Ops:
  0.6 36.3 %collective-permute-start = (bf16[5,256,640]{2,1,0:T(8,128)(2,1)}, bf16[5,256,640]{2,1,0:T(8,128)(2,1)}, u32[]{:S(2)}, u32[]{:S(2)}) collective-permute-start(bf16[5,256,640]{2,1,0:T(8,128)(2,1)} %bitcast.16), channel_id=1, source_target_pairs={{0,1},{1,0},{2,3},{3,2},{4,5},{5,4},{6,7},{7,6},{8,9},{9,8},{10,11... | collective-permute-start | bytes 4915208 | tf_op jit(solution)/shard_map/ppermute | solution.py:261
  1.7 0.7 %copy-start.2 = (s32[640]{0:T(1024)S(1)}, s32[640]{0:T(1024)}, u32[]{:S(2)}) copy-start(s32[640]{0:T(1024)} %param.6) | copy-start | bytes 7684
  5.5 0.7 %copy-start.1 = (bf16[1024,128]{1,0:T(8,128)(2,1)}, bf16[1024,128]{1,0:T(8,128)(2,1)S(1)}, u32[]{:S(2)}) copy-start(bf16[1024,128]{1,0:T(8,128)(2,1)S(1)} %get-tuple-element.6) | copy-start | bytes 786436
  6.2 30.7 %all-to-all-start = ((bf16[128,8,128]{2,1,0:T(8,128)(2,1)}), bf16[128,8,128]{2,1,0:T(8,128)(2,1)S(1)}, u32[]{:S(2)}, u32[]{:S(2)}) async-start(bf16[128,8,128]{2,1,0:T(8,128)(2,1)} %bitcast.22), calls=%async_computation | async-start | bytes 524288 | tf_op jit(solution)/shard_map/all_to_all | solution.py:278
  36.9 1.4 %copy-start = (bf16[5,1,256,640]{3,2,1,0:T(8,128)(2,1)S(1)}, bf16[5,1,256,640]{3,2,1,0:T(8,128)(2,1)}, u32[]{:S(2)}) copy-start(bf16[5,1,256,640]{3,2,1,0:T(8,128)(2,1)} %param.5) | copy-start | bytes 4915204
